TPU v7x, 64 devices: a 2x2x8 block of a 4x4x8 slice. The times are simulated.
64 devices in a mesh: rep: 8 (over x, y, core), dp: 8 (over z).
Axes of the slice: x: 2, y: 2, z: 8, core: 2. Of those that a mesh axis runs over, the one named last changes fastest.
The devices are a block of a 4x4x8 slice.
Arguments:
- g_w_gate: bfloat16 [64, 2, 512, 4096], P(('rep', 'dp')), parts along dimension 0
- g_w_up: bfloat16 [64, 2, 512, 4096], P(('rep', 'dp')), parts along dimension 0
- g_w_down: bfloat16 [64, 2, 4096, 512], P(('rep', 'dp')), parts along dimension 0
- w_gate: bfloat16 [2, 512, 4096], replicated
- w_up: bfloat16 [2, 512, 4096], replicated
- w_down: bfloat16 [2, 4096, 512], replicated
- m_w_gate: float32 [2, 512, 4096], P(None, 'dp')
- m_w_up: float32 [2, 512, 4096], P(None, 'dp')
- m_w_down: float32 [2, 4096, 512], P(None, 'dp')
- v_w_gate: float32 [2, 512, 4096], P(None, 'dp')
- v_w_up: float32 [2, 512, 4096], P(None, 'dp')
- v_w_down: float32 [2, 4096, 512], P(None, 'dp')
Outputs:
- output 1: bfloat16 [16, 512, 4096], P('rep'), parts along dimension 0
- output 2: bfloat16 [16, 512, 4096], P('rep'), parts along dimension 0
- output 3: bfloat16 [16, 4096, 512], P('rep'), parts along dimension 0
- output 4: float32 [16, 512, 4096], P('rep', 'dp'), parts along dimension 0
- output 5: float32 [16, 512, 4096], P('rep', 'dp'), parts along dimension 0
- output 6: float32 [16, 4096, 512], P('rep', 'dp'), parts along dimension 0
- output 7: float32 [16, 512, 4096], P('rep', 'dp'), parts along dimension 0
- output 8: float32 [16, 512, 4096], P('rep', 'dp'), parts along dimension 0
- output 9: float32 [16, 4096, 512], P('rep', 'dp'), parts along dimension 0
There are 8 independent parts. A program takes and returns all parts, laid end to end along the dimension named above; an argument that names none is the same for every part.
All inputs are finite; a program needn't handle non-finite values.
Results may differ from a plain program's by a relative error of at most 0.022.
Values are sent between devices in bfloat16 or wider.
A program may use at most 768 MiB of HBM per device.

v0:
```python
import jax
import jax.numpy as jnp
from jax import lax
from jax.sharding import PartitionSpec as P


def adamw(w, m, v, g):
    m = 0.9 * m + 0.1 * g
    v = 0.95 * v + 0.05 * g * g
    step = m * lax.rsqrt(v + 1e-8) + 0.1 * w
    return (w - 0.02 * step).astype(jnp.bfloat16), m, v


def clipped(gradients, sum_of_squares, count):
    factor = jnp.minimum(1.0, 0.5 * lax.rsqrt(sum_of_squares / count + 1e-30))
    return [g * factor for g in gradients]


def solution(mesh):
    def step(*arrays):
        terms, weights, m, v = (arrays[i : i + 3] for i in (0, 3, 6, 9))
        gradients = [lax.psum_scatter(t[0], "dp", scatter_dimension=1, tiled=True).astype(jnp.float32) for t in terms]
        squares = lax.psum(sum(jnp.sum(g * g) for g in gradients), "dp")
        gradients = clipped(gradients, squares, lax.psum(1, "dp") * sum(g.size for g in gradients))
        me = lax.axis_index("dp")
        own = [lax.dynamic_slice_in_dim(w, me * one.shape[1], one.shape[1], 1).astype(jnp.float32) for w, one in zip(weights, m, strict=True)]
        new = [adamw(w, m, v, g) for w, m, v, g in zip(own, m, v, gradients, strict=True)]
        whole = [lax.all_gather(one[0], "dp", axis=1, tiled=True) for one in new]
        return (*whole, *(one[1] for one in new), *(one[2] for one in new))

    all_of, cut = P(None, None, None), P(None, "dp", None)
    return jax.shard_map(
        step,
        mesh=mesh,
        in_specs=(P(("rep", "dp"), None, None, None),) * 3 + (all_of,) * 3 + (cut,) * 6,
        out_specs=(P("rep", None, None),) * 3 + (P("rep", "dp", None),) * 6,
        check_vma=False,
    )
```

profile of v0, /device:TPU:21, one launch (start us, length us, event | category | flops | bytes accessed | tf_op | source)
XLA Modules:
  0.0 620.9 jit_solution(13459879690127252349)
XLA Ops:
  7.3 0.7 reduce-scatter.4.cloned.1.call-update
  8.0 0.1 reduce-scatter.6.cloned.1.call-start
  8.1 0.7 reduce-scatter.6.cloned.1.call-update
  8.8 0.1 reduce-scatter.8.cloned.1.call-start
  8.9 0.7 reduce-scatter.8.cloned.1.call-update
  9.6 0.1 all-gather.8.cloned.1.call-start
  9.7 96.8 %reduce-scatter.4.cloned.1.call-done = bf16[2,64,4096]{2,1,0:T(8,128)(2,1)} async-done(((bf16[2,512,4096]{2,1,0:T(8,128)(2,1)}), bf16[2,64,4096]{2,1,0:T(8,128)(2,1)}) %reduce-scatter.4.cloned.1.call-update) | async-done | bytes 1048592 | tf_op jit(solution)/shard_map/reduce_scatter | solution.py:22
  106.4 2.4 fusion.9
  108.8 90.3 %reduce-scatter.6.cloned.1.call-done = bf16[2,64,4096]{2,1,0:T(8,128)(2,1)} async-done(((bf16[2,512,4096]{2,1,0:T(8,128)(2,1)}), bf16[2,64,4096]{2,1,0:T(8,128)(2,1)}) %reduce-scatter.6.cloned.1.call-update) | async-done | bytes 1048592 | tf_op jit(solution)/shard_map/reduce_scatter | solution.py:22
  199.1 2.4 fusion.10
  202.7 89.0 %reduce-scatter.8.cloned.1.call-done = bf16[2,512,512]{2,1,0:T(8,128)(2,1)} async-done(((bf16[2,4096,512]{2,1,0:T(8,128)(2,1)}), bf16[2,512,512]{2,1,0:T(8,128)(2,1)}) %reduce-scatter.8.cloned.1.call-update) | async-done | bytes 1048592 | tf_op jit(solution)/shard_map/reduce_scatter | solution.py:22
  291.7 2.4 fusion.11
  294.7 12.4 %psum.7 = f32[]{:T(128)} all-reduce(f32[]{:T(128)S(6)} %add.65), channel_id=1, replica_groups=mesh['rep'=8,'dp'=8] {'dp'}, use_global_device_ids=true, to_apply=%region_6.0 | all-reduce | flops 1 | bytes 8 | tf_op jit(solution)/shard_map/psum | solution.py:23
  307.8 6.0 fusion.17
  313.8 0.1 all-gather.4.cloned.1.call-start
  313.9 5.6 fusion.8
  319.6 0.1 all-gather.6.cloned.1.call-start
  319.7 5.5 fusion.14
  325.2 83.0 %all-gather.8.cloned.1.call-done = bf16[2,4096,512]{2,1,0:T(8,128)(2,1)} async-done(((bf16[2,512,512]{2,1,0:T(8,128)(2,1)}), bf16[2,4096,512]{2,1,0:T(8,128)(2,1)}) %all-gather.8.cloned.1.call-update) | async-done | bytes 8388624 | tf_op jit(solution)/shard_map/all_gather | solution.py:28
  408.3 91.3 %all-gather.4.cloned.1.call-done = bf16[2,512,4096]{2,1,0:T(8,128)(2,1)} async-done(((bf16[2,64,4096]{2,1,0:T(8,128)(2,1)}), bf16[2,512,4096]{2,1,0:T(8,128)(2,1)}) %all-gather.4.cloned.1.call-update) | async-done | bytes 8388624 | tf_op jit(solution)/shard_map/all_gather | solution.py:28
  499.6 91.3 %all-gather.6.cloned.1.call-done = bf16[2,512,4096]{2,1,0:T(8,128)(2,1)} async-done(((bf16[2,64,4096]{2,1,0:T(8,128)(2,1)}), bf16[2,512,4096]{2,1,0:T(8,128)(2,1)}) %all-gather.6.cloned.1.call-update) | async-done | bytes 8388624 | tf_op jit(solution)/shard_map/all_gather | solution.py:28
  590.9 7.9 %copy.24 = bf16[2,512,4096]{2,1,0:T(8,128)(2,1)} copy(bf16[2,512,4096]{2,1,0:T(8,128)(2,1)} %all-gather.4.cloned.1.call-done) | data formatting | bytes 16777216
  598.8 7.9 %copy.25 = bf16[2,512,4096]{2,1,0:T(8,128)(2,1)} copy(bf16[2,512,4096]{2,1,0:T(8,128)(2,1)} %all-gather.6.cloned.1.call-done) | data formatting | bytes 16777216
  606.7 7.3 %copy.26 = bf16[2,4096,512]{2,1,0:T(8,128)(2,1)} copy(bf16[2,4096,512]{2,1,0:T(8,128)(2,1)} %all-gather.8.cloned.1.call-done) | data formatting | bytes 16777216
  (8 shorter events, 0.2 us)
Async XLA Ops:
  7.2 99.3 %reduce-scatter.4.cloned.1.call-start = ((), (), s32[]{:S(2)}) async-start(), calls=%async_computation.3 | async-start | bytes 9437184 | tf_op jit(solution)/shard_map/reduce_scatter | solution.py:22
  8.0 191.1 %reduce-scatter.6.cloned.1.call-start = ((), (), s32[]{:S(2)}) async-start(), calls=%async_computation.4 | async-start | bytes 9437184 | tf_op jit(solution)/shard_map/reduce_scatter | solution.py:22
  8.8 282.9 %reduce-scatter.8.cloned.1.call-start = ((), (), s32[]{:S(2)}) async-start(), calls=%async_computation.5 | async-start | bytes 9437184 | tf_op jit(solution)/shard_map/reduce_scatter | solution.py:22
  9.6 398.7 %all-gather.8.cloned.1.call-start = ((), (), s32[]{:S(2)}) async-start(), calls=%async_computation.8 | async-start | bytes 9437184 | tf_op jit(solution)/shard_map/all_gather | solution.py:28
  307.8 6.1 copy-start.1
  313.8 185.7 %all-gather.4.cloned.1.call-start = ((), (), s32[]{:S(2)}) async-start(), calls=%async_computation.6 | async-start | bytes 9437184 | tf_op jit(solution)/shard_map/all_gather | solution.py:28
  313.9 5.7 copy-start
  319.6 271.3 %all-gather.6.cloned.1.call-start = ((), (), s32[]{:S(2)}) async-start(), calls=%async_computation.7 | async-start | bytes 9437184 | tf_op jit(solution)/shard_map/all_gather | solution.py:28
Sparse Core Ops, SparseCore 0:
  10.4 96.0 reduce-scatter.3
  108.8 90.2 reduce-scatter.5
  201.4 90.2 reduce-scatter.7
  314.0 94.2 all-gather.7
  410.3 89.2 all-gather.3
  501.6 89.2 all-gather.5
where the time goes:
time: 621 us
  waiting for transfers between devices  544 us (88%)
  other arithmetic  24.2 us (4%)
  local copies, waits for them, and re-layouts  23.1 us (4%)
  between operations  16.8 us (3%)
  blocking collectives  12.4 us (2%)
    reduce_scatter x3, waiting for transfers between devices, step(): lax.psum_scatter(t[0], 'dp', scatter_dimension=1, tiled=True)  276 us
    all_gather x3, waiting for transfers between devices, step(): whole = [lax.all_gather(one[0], 'dp', axis=1, tiled=True) for one in new]  266 us
    unnamed x7, local copies, waits for them, and re-layouts  23.1 us
    convert_element_type x3, other arithmetic, adamw(): return ((w - 0.02 * step).astype(jnp.bfloat16), m, v)  17.1 us
  transfers between devices with their start and end apart: 6, of which 6 were waited for; matrix products, arithmetic and copies ran while one was open for 3% of the time, Pallas kernels for 0%

commit v1 on v0

v1 whole, which is shorter than its diff:
```python
import functools

import jax
import jax.numpy as jnp
from jax import lax
from jax.experimental import pallas as pl
from jax.experimental.pallas import tpu as pltpu
from jax.sharding import PartitionSpec as P

MESH = pl.DeviceIdType.MESH
WAYS = 2


def adamw(w, m, v, g):
    m = 0.9 * m + 0.1 * g
    v = 0.95 * v + 0.05 * g * g
    step = m * lax.rsqrt(v + 1e-8) + 0.1 * w
    return (w - 0.02 * step).astype(jnp.bfloat16), m, v


def kernel(n, *refs):
    g, w, m, v = (refs[i : i + 3] for i in (0, 3, 6, 9))
    out, m_new, v_new = (refs[i : i + 3] for i in (12, 15, 18))
    terms, w_own = refs[21:24], refs[24:27]
    squares, send_sem, sum_sem, whole_sem, term_sem, own_sem, sq_send, sq_recv = refs[27:35]
    layers = out[0].shape[0]
    me = lax.axis_index("dp")
    chunks = [(which, layer) for which in range(3) for layer in range(layers)]
    own = [ref.shape[1] // n for ref in out]
    half = [rows // WAYS for rows in own]
    to = (lax.rem(me + 1, n), lax.rem(me + n - 1, n))
    sign = (1, -1)

    def rows(which, block, way):
        return pl.ds(pl.multiple_of(block * own[which] + way * half[which], half[which]), half[which])

    def block_of(way, back):
        return lax.rem(me - sign[way] * back + 2 * n, n)

    def term_copy(way, step, c):
        which, layer = chunks[c]
        slot = lax.rem(step, 2)
        return pltpu.make_async_copy(
            g[which].at[0, layer, rows(which, block_of(way, step + 2), way)],
            terms[which].at[way, slot, layer],
            term_sem.at[way, slot, c],
        )

    def send(way, c, src, place, sem):
        return pltpu.make_async_remote_copy(
            src_ref=src,
            dst_ref=place,
            send_sem=send_sem.at[way, c],
            recv_sem=sem,
            device_id={"dp": to[way]},
            device_id_type=MESH,
        )

    every = [(c, way) for c in range(len(chunks)) for way in range(WAYS)]

    for c, way in every:
        term_copy(way, 0, c).start()
    for c, way in every:
        term_copy(way, 1, c).start()
    barrier = pltpu.get_barrier_semaphore()
    for k in range(1, n):
        pl.semaphore_signal(barrier, inc=1, device_id={"dp": lax.rem(me + k, n)}, device_id_type=MESH)
    pl.semaphore_wait(barrier, n - 1)

    def sum_send(way, step, c):
        which, layer = chunks[c]
        place = out[which].at[layer, rows(which, block_of(way, step + 1), way)]
        return send(way, c, place, place, sum_sem.at[way, step, c])

    for c, way in every:
        which, layer = chunks[c]
        at = rows(which, block_of(way, 1), way)
        send(way, c, g[which].at[0, layer, at], out[which].at[layer, at], sum_sem.at[way, 0, c]).start()

    own_loads = []
    for which in range(3):
        mine = pl.ds(pl.multiple_of(me * own[which], own[which]), own[which])
        own_loads += [
            pltpu.make_async_copy(w[which].at[:, mine], w_own[which], own_sem.at[0, which]),
            pltpu.make_async_copy(m[which], m_new[which], own_sem.at[1, which]),
            pltpu.make_async_copy(v[which], v_new[which], own_sem.at[2, which]),
        ]
    for copy in own_loads:
        copy.start()

    def add(way, step, c):
        which, layer = chunks[c]
        place = out[which].at[layer, rows(which, block_of(way, step + 2), way)]
        send(way, c, place, place, sum_sem.at[way, step, c]).wait_recv()
        term_copy(way, step, c).wait()
        term = terms[which][way, lax.rem(step, 2), layer]
        total = (place[...].astype(jnp.float32) + term.astype(jnp.float32)).astype(jnp.bfloat16)
        place[...] = total
        return total

    def sum_step(step, _):
        for c, way in every:
            add(way, step, c)
            sum_send(way, step, c).wait_send()
            sum_send(way, step + 1, c).start()

            @pl.when(step + 2 <= n - 2)
            def _():
                term_copy(way, step + 2, c).start()

        return 0

    lax.fori_loop(0, n - 2, sum_step, 0)
    tile = jnp.zeros((8, 128), jnp.float32)
    for c, way in every:
        total = add(way, n - 2, c).astype(jnp.float32)
        square = total * total
        square = jnp.sum(square.reshape(square.shape[0] // 8, 8, square.shape[1]), axis=0)
        for i in range(square.shape[1] // 128):
            tile = tile + square[:, i * 128 : (i + 1) * 128]
    for c, way in every:
        sum_send(way, n - 2, c).wait_send()

    squares[me] = tile
    tells = [
        pltpu.make_async_remote_copy(
            src_ref=squares.at[me],
            dst_ref=squares.at[me],
            send_sem=sq_send.at[k - 1],
            recv_sem=sq_recv.at[k - 1],
            device_id={"dp": lax.rem(me + k, n)},
            device_id_type=MESH,
        )
        for k in range(1, n)
    ]
    for tell in tells:
        tell.start()
    for copy in own_loads:
        copy.wait()
    for k in range(1, n):
        theirs = squares.at[lax.rem(me + n - k, n)]
        pltpu.make_async_remote_copy(
            src_ref=theirs, dst_ref=theirs, send_sem=sq_send.at[k - 1], recv_sem=sq_recv.at[k - 1],
            device_id={"dp": lax.rem(me + k, n)}, device_id_type=MESH,
        ).wait_recv()
    count = n * sum(ref.size for ref in m)
    total = jnp.sum(jnp.sum(squares[...], axis=0), axis=(0, 1), keepdims=True)
    factor = jnp.minimum(1.0, 0.5 * lax.rsqrt(total / count + 1e-30))

    def whole_send(way, step, c):
        which, layer = chunks[c]
        place = out[which].at[layer, rows(which, block_of(way, step), way)]
        return send(way, c, place, place, whole_sem.at[way, step, c])

    for c, way in every:
        which, layer = chunks[c]
        here = pl.ds(way * half[which], half[which])
        place = out[which].at[layer, rows(which, me, way)]
        new = adamw(
            w_own[which][layer, here].astype(jnp.float32),
            m_new[which][layer, here],
            v_new[which][layer, here],
            place[...].astype(jnp.float32) * factor,
        )
        place[...], m_new[which][layer, here], v_new[which][layer, here] = new
        whole_send(way, 0, c).start()

    def arrived(way, step, c):
        which, layer = chunks[c]
        place = out[which].at[layer, rows(which, block_of(way, step + 1), way)]
        send(way, c, place, place, whole_sem.at[way, step, c]).wait_recv()

    def whole_step(step, _):
        for c, way in every:
            arrived(way, step, c)
            whole_send(way, step, c).wait_send()
            whole_send(way, step + 1, c).start()
        return 0

    lax.fori_loop(0, n - 2, whole_step, 0)
    for c, way in every:
        arrived(way, n - 2, c)
    for c, way in every:
        whole_send(way, n - 2, c).wait_send()
    for tell in tells:
        tell.wait_send()


def put_out(*refs):
    copies = [pltpu.make_async_copy(refs[i], refs[9 + i], refs[18].at[i]) for i in range(9)]
    for copy in copies:
        copy.start()
    for copy in copies:
        copy.wait()


def solution(mesh):
    n = mesh.shape["dp"]

    def step(*arrays):
        terms, weights, m, v = (arrays[i : i + 3] for i in (0, 3, 6, 9))
        layers = weights[0].shape[0]
        count = 3 * layers
        anywhere = pl.BlockSpec(memory_space=pl.ANY)
        half = [(x.shape[1] // n // WAYS, x.shape[2]) for x in weights]
        made = pl.pallas_call(
            functools.partial(kernel, n),
            out_shape=[pltpu.VMEM(x.shape, x.dtype) for x in (*weights, *m, *v)],
            in_specs=[anywhere] * 12,
            out_specs=[pl.BlockSpec(memory_space=pltpu.VMEM)] * 9,
            scratch_shapes=[
                *(pltpu.VMEM((WAYS, 2, layers, *h), jnp.bfloat16) for h in half),
                *(pltpu.VMEM((layers, x.shape[1] // n, x.shape[2]), jnp.bfloat16) for x in weights),
                pltpu.VMEM((n, 8, 128), jnp.float32),
                pltpu.SemaphoreType.DMA((WAYS, count)),
                pltpu.SemaphoreType.DMA((WAYS, n - 1, count)),
                pltpu.SemaphoreType.DMA((WAYS, n - 1, count)),
                pltpu.SemaphoreType.DMA((WAYS, 2, count)),
                pltpu.SemaphoreType.DMA((3, 3)),
                pltpu.SemaphoreType.DMA((n - 1,)),
                pltpu.SemaphoreType.DMA((n - 1,)),
            ],
            compiler_params=pltpu.CompilerParams(
                collective_id=0, has_side_effects=True, vmem_limit_bytes=16 * 2**20
            ),
            name="step_end",
        )(*terms, *weights, *m, *v)
        return pl.pallas_call(
            put_out,
            out_shape=[jax.ShapeDtypeStruct(x.shape, x.dtype) for x in (*weights, *m, *v)],
            in_specs=[pl.BlockSpec(memory_space=pltpu.VMEM)] * 9,
            out_specs=[anywhere] * 9,
            scratch_shapes=[pltpu.SemaphoreType.DMA((9,))],
            compiler_params=pltpu.CompilerParams(vmem_limit_bytes=16 * 2**20),
            name="put_out",
        )(*made)

    all_of, cut = P(None, None, None), P(None, "dp", None)
    return jax.shard_map(
        step,
        mesh=mesh,
        in_specs=(P(("rep", "dp"), None, None, None),) * 3 + (all_of,) * 3 + (cut,) * 6,
        out_specs=(P("rep", None, None),) * 3 + (P("rep", "dp", None),) * 6,
        check_vma=False,
    )
```

time: 621 us -> 503 us (0.81)
  waiting for transfers between devices: 544 us -> 0 us
  Pallas kernels: 0 us -> 501 us
  other arithmetic: 24.2 us -> 0 us
  local copies, waits for them, and re-layouts: 23.1 us -> 0 us
  between operations: 16.8 us -> 0.65 us
  blocking collectives: 12.4 us -> 0 us
    pallas_call x0 -> x2, Pallas kernels: none -> 501 us  [the longest x1 489 us: step(): pl.pallas_call(functools.partial(kernel, n), out_shape=[pltpu.VMEM(x.shap...]
    reduce_scatter x3 -> x0, waiting for transfers between devices: 276 us -> none  [step(): lax.psum_scatter(t[0], 'dp', scatter_dimension=1, tiled=True)]
    all_gather x3 -> x0, waiting for transfers between devices: 266 us -> none  [step(): whole = [lax.all_gather(one[0], 'dp', axis=1, tiled=True) for one in new]]
    unnamed x7 -> x0, local copies, waits for them, and re-layouts: 23.1 us -> none
    convert_element_type x3 -> x0, other arithmetic: 17.1 us -> none  [adamw(): return ((w - 0.02 * step).astype(jnp.bfloat16), m, v)]
    psum x1 -> x0, blocking collectives: 12.4 us -> none  [step(): squares = lax.psum(sum((jnp.sum(g * g) for g in gradients)), 'dp')]
    reduce_sum x3 -> x0, other arithmetic: 7.11 us -> none  [step(): squares = lax.psum(sum((jnp.sum(g * g) for g in gradients)), 'dp')]
  transfers between devices with their start and end apart: 6 -> 0, of which waited for: 6 -> 0; matrix products, arithmetic and copies ran while one was open for 3% -> 0% of each run, Pallas kernels for 0% -> 0%
where the time goes in v1:
time: 503 us; the launch traced here: 502 us
  Pallas kernels  501 us (100%)
    pallas_call x1, Pallas kernels, step(): pl.pallas_call(functools.partial(kernel, n), out_shape=[pltpu.VMEM(x.shap...  489 us
    pallas_call x1, Pallas kernels, step(): pl.pallas_call(put_out, out_shape=[jax.ShapeDtypeStruct(x.shape, x.dtype)...  12.4 us

profile of v1, /device:TPU:21, one launch (start us, length us, event | category | flops | bytes accessed | tf_op | source)
XLA Modules:
  0.0 501.8 jit_solution(2369947043918673330)
XLA Ops:
  0.6 488.8 %step_end.1 = (bf16[2,512,4096]{2,1,0:T(8,128)(2,1)S(1)}, bf16[2,512,4096]{2,1,0:T(8,128)(2,1)S(1)}, bf16[2,4096,512]{2,1,0:T(8,128)(2,1)S(1)}, f32[2,64,4096]{2...) custom-call(bf16[1,2,512,4096]{3,2,1,0:T(8,128)(2,1)} %refs_0_.1, ...), custom_call_target="tpu_custom_call" | custom-call | tf_op jit(solution)/shard_map/step_end/pallas_call | solution.py:206
  489.5 12.4 %put_out.1 = (bf16[2,512,4096]{2,1,0:T(8,128)(2,1)}, bf16[2,512,4096]{2,1,0:T(8,128)(2,1)}, bf16[2,4096,512]{2,1,0:T(8,128)(2,1)}, f32[2,64,4096]{2,1,0:T(8,128)...) custom-call(bf16[2,512,4096]{2,1,0:T(8,128)(2,1)S(1)} %get-tuple-ele, ...), custom_call_target="tpu_custom_call" | custom-call | tf_op jit(solution)/shard_map/put_out/pallas_call | solution.py:228

commit v2 on v1

v2 whole, which is shorter than its diff:
```python
import functools

import jax
import jax.numpy as jnp
from jax import lax
from jax.experimental import pallas as pl
from jax.experimental.pallas import tpu as pltpu
from jax.sharding import PartitionSpec as P

MESH = pl.DeviceIdType.MESH
WAYS = 2
PARTS = 2
LAG = 22000


def adamw(w, m, v, g):
    m = 0.9 * m + 0.1 * g
    v = 0.95 * v + 0.05 * g * g
    step = m * lax.rsqrt(v + 1e-8) + 0.1 * w
    return (w - 0.02 * step).astype(jnp.bfloat16), m, v


class Ring:
    def __init__(self, n):
        self.n, self.me = n, lax.axis_index("dp")
        self.to = (lax.rem(self.me + 1, n), lax.rem(self.me + n - 1, n))

    def block_of(self, way, back):
        return lax.rem(self.me + (-back, back)[way] + 2 * self.n, self.n)

    def send(self, way, src, place, send_sem, recv_sem):
        return pltpu.make_async_remote_copy(
            src_ref=src,
            dst_ref=place,
            send_sem=send_sem,
            recv_sem=recv_sem,
            device_id={"dp": self.to[way]},
            device_id_type=MESH,
        )


def gather(ring, every, place_of, send_sem, recv_sem):
    def forward(way, step, c):
        place = place_of(way, ring.block_of(way, step), c)
        return ring.send(way, place, place, send_sem.at[way, c], recv_sem.at[way, step, c])

    def arrived(way, step, c):
        place = place_of(way, ring.block_of(way, step + 1), c)
        ring.send(way, place, place, send_sem.at[way, c], recv_sem.at[way, step, c]).wait_recv()

    def one(step, _):
        for c, way in every:
            arrived(way, step, c)
            forward(way, step, c).wait_send()
            forward(way, step + 1, c).start()
        return 0

    last = ring.n - 2
    lax.fori_loop(0, last, one, 0)
    for c, way in every:
        arrived(way, last, c)
    for c, way in every:
        forward(way, last, c).wait_send()


def sum_and_step(n, *refs):
    g, w, m, v = (refs[i : i + 3] for i in (0, 3, 6, 9))
    gate, up, own_down = refs[12:15]
    m_new, v_new = refs[15:18], refs[18:21]
    down, terms, w_own = refs[21], refs[22:25], refs[25:28]
    squares, send_sem, sum_sem, whole_sem, term_sem, own_sem, sq_send, sq_recv = refs[28:36]
    out = (gate, up, down)
    layers = down.shape[0]
    ring = Ring(n)
    me, block_of = ring.me, ring.block_of
    chunks = [(which, layer) for which in range(3) for layer in range(layers)]
    every = [(c, way) for c in range(len(chunks)) for way in range(WAYS)]
    own = [ref.shape[1] // n for ref in out]
    half = [rows // WAYS for rows in own]

    def rows(which, block, way):
        return pl.ds(pl.multiple_of(block * own[which] + way * half[which], half[which]), half[which])

    def place_of(way, block, c):
        which, layer = chunks[c]
        return out[which].at[layer, rows(which, block, way)]

    def term_copy(way, step, c):
        which, layer = chunks[c]
        slot = lax.rem(step, 2)
        return pltpu.make_async_copy(
            g[which].at[0, layer, rows(which, block_of(way, step + 2), way)],
            terms[which].at[way, slot, layer],
            term_sem.at[way, slot, c],
        )

    for step in range(2):
        for c, way in every:
            term_copy(way, step, c).start()
    barrier = pltpu.get_barrier_semaphore()
    for k in range(1, n):
        pl.semaphore_signal(barrier, inc=1, device_id={"dp": lax.rem(me + k, n)}, device_id_type=MESH)
    pl.semaphore_wait(barrier, n - 1)
    pl.delay(lax.rem(lax.axis_index("rep"), 2) * LAG)

    def sum_send(way, step, c):
        place = place_of(way, block_of(way, step + 1), c)
        return ring.send(way, place, place, send_sem.at[way, c], sum_sem.at[way, step, c])

    for c, way in every:
        which, layer = chunks[c]
        block = block_of(way, 1)
        src = g[which].at[0, layer, rows(which, block, way)]
        ring.send(way, src, place_of(way, block, c), send_sem.at[way, c], sum_sem.at[way, 0, c]).start()

    own_loads = []
    for which in range(3):
        mine = pl.ds(pl.multiple_of(me * own[which], own[which]), own[which])
        own_loads += [
            pltpu.make_async_copy(w[which].at[:, mine], w_own[which], own_sem.at[0, which]),
            pltpu.make_async_copy(m[which], m_new[which], own_sem.at[1, which]),
            pltpu.make_async_copy(v[which], v_new[which], own_sem.at[2, which]),
        ]
    for copy in own_loads:
        copy.start()

    def add(way, step, c):
        which, layer = chunks[c]
        place = place_of(way, block_of(way, step + 2), c)
        ring.send(way, place, place, send_sem.at[way, c], sum_sem.at[way, step, c]).wait_recv()
        term_copy(way, step, c).wait()
        term = terms[which][way, lax.rem(step, 2), layer]
        total = (place[...].astype(jnp.float32) + term.astype(jnp.float32)).astype(jnp.bfloat16)
        place[...] = total
        return total

    def sum_step(step, _):
        for c, way in every:
            add(way, step, c)
            sum_send(way, step, c).wait_send()
            sum_send(way, step + 1, c).start()

            @pl.when(step + 2 <= n - 2)
            def _():
                term_copy(way, step + 2, c).start()

        return 0

    lax.fori_loop(0, n - 2, sum_step, 0)
    tile = jnp.zeros((8, 128), jnp.float32)
    for c, way in every:
        total = add(way, n - 2, c).astype(jnp.float32)
        square = total * total
        square = jnp.sum(square.reshape(square.shape[0] // 8, 8, square.shape[1]), axis=0)
        for i in range(square.shape[1] // 128):
            tile = tile + square[:, i * 128 : (i + 1) * 128]
    for c, way in every:
        sum_send(way, n - 2, c).wait_send()

    squares[me] = tile

    def tell(k, whose):
        return pltpu.make_async_remote_copy(
            src_ref=squares.at[whose],
            dst_ref=squares.at[whose],
            send_sem=sq_send.at[k - 1],
            recv_sem=sq_recv.at[k - 1],
            device_id={"dp": lax.rem(me + k, n)},
            device_id_type=MESH,
        )

    for k in range(1, n):
        tell(k, me).start()
    for copy in own_loads:
        copy.wait()
    for k in range(1, n):
        tell(k, lax.rem(me + n - k, n)).wait_recv()
    count = n * sum(ref.size for ref in m)
    total = jnp.sum(jnp.sum(squares[...], axis=0), axis=(0, 1), keepdims=True)
    factor = jnp.minimum(1.0, 0.5 * lax.rsqrt(total / count + 1e-30))

    gathered = [(c, way) for c, way in every if chunks[c][0] < 2]
    for c, way in every:
        which, layer = chunks[c]
        here = pl.ds(way * half[which], half[which])
        place = place_of(way, me, c)
        new, m_new[which][layer, here], v_new[which][layer, here] = adamw(
            w_own[which][layer, here].astype(jnp.float32),
            m_new[which][layer, here],
            v_new[which][layer, here],
            place[...].astype(jnp.float32) * factor,
        )
        if (c, way) in gathered:
            place[...] = new
            ring.send(way, place, place, send_sem.at[way, c], whole_sem.at[way, 0, c]).start()
        else:
            own_down[layer, here] = new
    gather(ring, gathered, place_of, send_sem, whole_sem)
    for k in range(1, n):
        tell(k, me).wait_send()


def gather_last(n, new, after, out, send_sem, recv_sem):
    del after
    ring = Ring(n)
    layers, own = new.shape[:2]
    size = own // WAYS // PARTS
    every = [(c, way) for c in range(layers * PARTS) for way in range(WAYS)]

    def place_of(way, block, c):
        first = block * own + (way * PARTS + c % PARTS) * size
        return out.at[c // PARTS, pl.ds(pl.multiple_of(first, size), size)]

    barrier = pltpu.get_barrier_semaphore()
    for to in ring.to:
        pl.semaphore_signal(barrier, inc=1, device_id={"dp": to}, device_id_type=MESH)
    pl.semaphore_wait(barrier, WAYS)
    for c, way in every:
        src = new.at[c // PARTS, pl.ds((way * PARTS + c % PARTS) * size, size)]
        ring.send(way, src, place_of(way, ring.me, c), send_sem.at[way, c], recv_sem.at[way, 0, c]).start()
    out[:, pl.ds(pl.multiple_of(ring.me * own, own), own)] = new[...]

    gather(ring, every, place_of, send_sem, recv_sem)


def put_out(arrays, *refs):
    sem = refs[-1]
    copies = [pltpu.make_async_copy(refs[i], refs[arrays + i], sem.at[i]) for i in range(arrays)]
    for copy in copies:
        copy.start()
    if len(refs) > 2 * arrays + 1:
        refs[2 * arrays][...] = jnp.zeros_like(refs[2 * arrays])
    for copy in copies:
        copy.wait()


def solution(mesh):
    n = mesh.shape["dp"]

    def step(*arrays):
        terms, weights, m, v = (arrays[i : i + 3] for i in (0, 3, 6, 9))
        layers = weights[0].shape[0]
        count = 3 * layers
        hbm = pl.BlockSpec(memory_space=pltpu.HBM)
        vmem = pl.BlockSpec(memory_space=pltpu.VMEM)
        cut = [(layers, x.shape[1] // n, x.shape[2]) for x in weights]
        half = [(rows // WAYS, columns) for _, rows, columns in cut]
        moments = [pltpu.VMEM(x.shape, x.dtype) for x in (*m, *v)]
        gate, up, own_down, *moments = pl.pallas_call(
            functools.partial(sum_and_step, n),
            out_shape=[
                *(pltpu.VMEM(x.shape, x.dtype) for x in weights[:2]),
                pltpu.VMEM(cut[2], weights[2].dtype),
                *moments,
            ],
            in_specs=[hbm] * 12,
            out_specs=[vmem] * 9,
            scratch_shapes=[
                pltpu.VMEM(weights[2].shape, jnp.bfloat16),
                *(pltpu.VMEM((WAYS, 2, layers, *h), jnp.bfloat16) for h in half),
                *(pltpu.VMEM(c, jnp.bfloat16) for c in cut),
                pltpu.VMEM((n, 8, 128), jnp.float32),
                pltpu.SemaphoreType.DMA((WAYS, count)),
                pltpu.SemaphoreType.DMA((WAYS, n - 1, count)),
                pltpu.SemaphoreType.DMA((WAYS, n - 1, count)),
                pltpu.SemaphoreType.DMA((WAYS, 2, count)),
                pltpu.SemaphoreType.DMA((3, 3)),
                pltpu.SemaphoreType.DMA((n - 1,)),
                pltpu.SemaphoreType.DMA((n - 1,)),
            ],
            compiler_params=pltpu.CompilerParams(
                collective_id=0, has_side_effects=True, vmem_limit_bytes=24 * 2**20
            ),
            name="sum_and_step",
        )(*terms, *weights, *m, *v)

        def put(limit, token, *some):
            return pl.pallas_call(
                functools.partial(put_out, len(some)),
                out_shape=[jax.ShapeDtypeStruct(x.shape, x.dtype) for x in some]
                + [jax.ShapeDtypeStruct((8, 128), jnp.float32)] * token,
                in_specs=[vmem] * len(some),
                out_specs=[hbm] * len(some) + [vmem] * token,
                scratch_shapes=[pltpu.SemaphoreType.DMA((len(some),))],
                compiler_params=pltpu.CompilerParams(vmem_limit_bytes=limit * 2**20),
                name="put_out",
            )(*some)

        gate, up, *moments, token = put(24, 1, gate, up, *moments)
        pieces = layers * PARTS
        down = pl.pallas_call(
            functools.partial(gather_last, n),
            out_shape=pltpu.VMEM(weights[2].shape, weights[2].dtype),
            in_specs=[vmem, vmem],
            out_specs=vmem,
            scratch_shapes=[
                pltpu.SemaphoreType.DMA((WAYS, pieces)),
                pltpu.SemaphoreType.DMA((WAYS, n - 1, pieces)),
            ],
            compiler_params=pltpu.CompilerParams(
                collective_id=1, has_side_effects=True, vmem_limit_bytes=24 * 2**20
            ),
            name="gather_last",
        )(own_down, token)
        (down,) = put(24, 0, down)
        return gate, up, down, *moments

    all_of, cut = P(None, None, None), P(None, "dp", None)
    return jax.shard_map(
        step,
        mesh=mesh,
        in_specs=(P(("rep", "dp"), None, None, None),) * 3 + (all_of,) * 3 + (cut,) * 6,
        out_specs=(P("rep", None, None),) * 3 + (P("rep", "dp", None),) * 6,
        check_vma=False,
    )
```

time: 503 us -> 489 us (0.972)
  Pallas kernels: 501 us -> 488 us
    pallas_call x2 -> x4, Pallas kernels: 501 us -> 488 us  [the longest x1 412 us: step(): pl.pallas_call(functools.partial(sum_and_step, n), out_shape=[*(pltpu.VME...]
where the time goes in v2:
time: 489 us
  Pallas kernels  488 us (100%)
    pallas_call x1, Pallas kernels, step(): pl.pallas_call(functools.partial(sum_and_step, n), out_shape=[*(pltpu.VME...  412 us
    pallas_call x1, Pallas kernels, step(): pl.pallas_call(functools.partial(gather_last, n), out_shape=pltpu.VMEM(we...  63.3 us
    pallas_call x2, Pallas kernels, put(): pl.pallas_call(functools.partial(put_out, len(some)), out_shape=[jax.Shap...  13.2 us

profile of v2, /device:TPU:21, one launch (start us, length us, event | category | flops | bytes accessed | tf_op | source)
XLA Modules:
  0.0 488.9 jit_solution(6330077871644526638)
XLA Ops:
  0.6 411.7 %sum_and_step.1 = (bf16[2,512,4096]{2,1,0:T(8,128)(2,1)S(1)}, bf16[2,512,4096]{2,1,0:T(8,128)(2,1)S(1)}, bf16[2,512,512]{2,1,0:T(8,128)(2,1)S(1)}, f32[2,64,4096...) custom-call(bf16[1,2,512,4096]{3,2,1,0:T(8,128)(2,1)} %refs_0_.1, ...), custom_call_target="tpu_custom_call" | custom-call | tf_op jit(solution)/shard_map/sum_and_step/pallas_call | solution.py:249
  412.3 9.8 %put_out.2 = (bf16[2,512,4096]{2,1,0:T(8,128)(2,1)}, bf16[2,512,4096]{2,1,0:T(8,128)(2,1)}, f32[2,64,4096]{2,1,0:T(8,128)}, f32[2,64,4096]{2,1,0:T(8,128)}, f32[...) custom-call(bf16[2,512,4096]{2,1,0:T(8,128)(2,1)S(1)} %get-tuple-ele, ...), custom_call_target="tpu_custom_call" | custom-call | tf_op jit(solution)/shard_map/put_out/pallas_call | solution.py:278
  422.2 63.3 %gather_last.1.refs_0_ = bf16[2,4096,512]{2,1,0:T(8,128)(2,1)S(1)} custom-call(bf16[2,512,512]{2,1,0:T(8,128)(2,1)S(1)} %get-tuple-element.37.new, f32[8,128]{1,0:T(8,128)S(1)} %get-tuple-element.38.after), custom_call_target="tpu_custom_call" | custom-call | tf_op jit(solution)/shard_map/gather_last/pallas_call | solution.py:291
  485.5 3.4 put_out.3

commit v3 on v2

--- a/solution.py
+++ b/solution.py
@@ -10,7 +10,7 @@
 MESH = pl.DeviceIdType.MESH
 WAYS = 2
 PARTS = 2
-LAG = 22000
+LAG = 25000
 
 
 def adamw(w, m, v, g):
@@ -94,13 +94,12 @@
             term_sem.at[way, slot, c],
         )
 
-    for step in range(2):
-        for c, way in every:
-            term_copy(way, step, c).start()
     barrier = pltpu.get_barrier_semaphore()
-    for k in range(1, n):
-        pl.semaphore_signal(barrier, inc=1, device_id={"dp": lax.rem(me + k, n)}, device_id_type=MESH)
-    pl.semaphore_wait(barrier, n - 1)
+    for to in ring.to:
+        pl.semaphore_signal(barrier, inc=1, device_id={"dp": to}, device_id_type=MESH)
+    for c, way in every:
+        term_copy(way, 0, c).start()
+    pl.semaphore_wait(barrier, WAYS)
     pl.delay(lax.rem(lax.axis_index("rep"), 2) * LAG)
 
     def sum_send(way, step, c):
@@ -113,6 +112,8 @@
         src = g[which].at[0, layer, rows(which, block, way)]
         ring.send(way, src, place_of(way, block, c), send_sem.at[way, c], sum_sem.at[way, 0, c]).start()
 
+    for c, way in every:
+        term_copy(way, 1, c).start()
     own_loads = []
     for which in range(3):
         mine = pl.ds(pl.multiple_of(me * own[which], own[which]), own[which])
@@ -158,23 +159,26 @@
         sum_send(way, n - 2, c).wait_send()
 
     squares[me] = tile
-
-    def tell(k, whose):
-        return pltpu.make_async_remote_copy(
-            src_ref=squares.at[whose],
-            dst_ref=squares.at[whose],
-            send_sem=sq_send.at[k - 1],
-            recv_sem=sq_recv.at[k - 1],
-            device_id={"dp": lax.rem(me + k, n)},
-            device_id_type=MESH,
-        )
-
-    for k in range(1, n):
-        tell(k, me).start()
+    hops = (n // 2, n - 1 - n // 2)
+
+    def tell(way, step):
+        place = squares.at[block_of(way, step)]
+        return ring.send(way, place, place, sq_send.at[way, step], sq_recv.at[way, step])
+
+    def told(way, step):
+        place = squares.at[block_of(way, step + 1)]
+        ring.send(way, place, place, sq_send.at[way, step], sq_recv.at[way, step]).wait_recv()
+
+    for way in range(WAYS):
+        tell(way, 0).start()
     for copy in own_loads:
         copy.wait()
-    for k in range(1, n):
-        tell(k, lax.rem(me + n - k, n)).wait_recv()
+    for step in range(max(hops)):
+        for way in range(WAYS):
+            if step < hops[way]:
+                told(way, step)
+            if step + 1 < hops[way]:
+                tell(way, step + 1).start()
     count = n * sum(ref.size for ref in m)
     total = jnp.sum(jnp.sum(squares[...], axis=0), axis=(0, 1), keepdims=True)
     factor = jnp.minimum(1.0, 0.5 * lax.rsqrt(total / count + 1e-30))
@@ -196,8 +200,9 @@
         else:
             own_down[layer, here] = new
     gather(ring, gathered, place_of, send_sem, whole_sem)
-    for k in range(1, n):
-        tell(k, me).wait_send()
+    for way in range(WAYS):
+        for step in range(hops[way]):
+            tell(way, step).wait_send()
 
 
 def gather_last(n, new, after, out, send_sem, recv_sem):
@@ -265,8 +270,8 @@
                 pltpu.SemaphoreType.DMA((WAYS, n - 1, count)),
                 pltpu.SemaphoreType.DMA((WAYS, 2, count)),
                 pltpu.SemaphoreType.DMA((3, 3)),
-                pltpu.SemaphoreType.DMA((n - 1,)),
-                pltpu.SemaphoreType.DMA((n - 1,)),
+                pltpu.SemaphoreType.DMA((WAYS, n - 1)),
+                pltpu.SemaphoreType.DMA((WAYS, n - 1)),
             ],
             compiler_params=pltpu.CompilerParams(
                 collective_id=0, has_side_effects=True, vmem_limit_bytes=24 * 2**20

time: 489 us -> 487 us (level)
  no operation moved by 1% of the time
where the time goes in v3:
time: 487 us
  Pallas kernels  487 us (100%)
    pallas_call x1, Pallas kernels, step(): pl.pallas_call(functools.partial(sum_and_step, n), out_shape=[*(pltpu.VME...  410 us
    pallas_call x1, Pallas kernels, step(): pl.pallas_call(functools.partial(gather_last, n), out_shape=pltpu.VMEM(we...  63.7 us
    pallas_call x2, Pallas kernels, put(): pl.pallas_call(functools.partial(put_out, len(some)), out_shape=[jax.Shap...  13.2 us

profile of v3, /device:TPU:21, one launch (start us, length us, event | category | flops | bytes accessed | tf_op | source)
XLA Modules:
  0.0 487.3 jit_solution(8223761894355563209)
XLA Ops:
  0.6 409.8 %sum_and_step.1 = (bf16[2,512,4096]{2,1,0:T(8,128)(2,1)S(1)}, bf16[2,512,4096]{2,1,0:T(8,128)(2,1)S(1)}, bf16[2,512,512]{2,1,0:T(8,128)(2,1)S(1)}, f32[2,64,4096...) custom-call(bf16[1,2,512,4096]{3,2,1,0:T(8,128)(2,1)} %refs_0_.1, ...), custom_call_target="tpu_custom_call" | custom-call | tf_op jit(solution)/shard_map/sum_and_step/pallas_call | solution.py:254
  410.4 9.8 %put_out.2 = (bf16[2,512,4096]{2,1,0:T(8,128)(2,1)}, bf16[2,512,4096]{2,1,0:T(8,128)(2,1)}, f32[2,64,4096]{2,1,0:T(8,128)}, f32[2,64,4096]{2,1,0:T(8,128)}, f32[...) custom-call(bf16[2,512,4096]{2,1,0:T(8,128)(2,1)S(1)} %get-tuple-ele, ...), custom_call_target="tpu_custom_call" | custom-call | tf_op jit(solution)/shard_map/put_out/pallas_call | solution.py:283
  420.3 63.7 %gather_last.1.refs_0_ = bf16[2,4096,512]{2,1,0:T(8,128)(2,1)S(1)} custom-call(bf16[2,512,512]{2,1,0:T(8,128)(2,1)S(1)} %get-tuple-element.37.new, f32[8,128]{1,0:T(8,128)S(1)} %get-tuple-element.38.after), custom_call_target="tpu_custom_call" | custom-call | tf_op jit(solution)/shard_map/gather_last/pallas_call | solution.py:296
  483.9 3.4 put_out.3

commit v4 on v3

--- a/solution.py
+++ b/solution.py
@@ -9,7 +9,7 @@
 
 MESH = pl.DeviceIdType.MESH
 WAYS = 2
-PARTS = 2
+PARTS = 1
 LAG = 25000
 
 
@@ -70,11 +70,9 @@
     down, terms, w_own = refs[21], refs[22:25], refs[25:28]
     squares, send_sem, sum_sem, whole_sem, term_sem, own_sem, sq_send, sq_recv = refs[28:36]
     out = (gate, up, down)
-    layers = down.shape[0]
     ring = Ring(n)
     me, block_of = ring.me, ring.block_of
-    chunks = [(which, layer) for which in range(3) for layer in range(layers)]
-    every = [(c, way) for c in range(len(chunks)) for way in range(WAYS)]
+    every = [(c, way) for c in range(len(out)) for way in range(WAYS)]
     own = [ref.shape[1] // n for ref in out]
     half = [rows // WAYS for rows in own]
 
@@ -82,15 +80,13 @@
         return pl.ds(pl.multiple_of(block * own[which] + way * half[which], half[which]), half[which])
 
     def place_of(way, block, c):
-        which, layer = chunks[c]
-        return out[which].at[layer, rows(which, block, way)]
+        return out[c].at[:, rows(c, block, way)]
 
     def term_copy(way, step, c):
-        which, layer = chunks[c]
         slot = lax.rem(step, 2)
         return pltpu.make_async_copy(
-            g[which].at[0, layer, rows(which, block_of(way, step + 2), way)],
-            terms[which].at[way, slot, layer],
+            g[c].at[0, :, rows(c, block_of(way, step + 2), way)],
+            terms[c].at[way, slot],
             term_sem.at[way, slot, c],
         )
 
@@ -107,9 +103,8 @@
         return ring.send(way, place, place, send_sem.at[way, c], sum_sem.at[way, step, c])
 
     for c, way in every:
-        which, layer = chunks[c]
         block = block_of(way, 1)
-        src = g[which].at[0, layer, rows(which, block, way)]
+        src = g[c].at[0, :, rows(c, block, way)]
         ring.send(way, src, place_of(way, block, c), send_sem.at[way, c], sum_sem.at[way, 0, c]).start()
 
     for c, way in every:
@@ -126,11 +121,10 @@
         copy.start()
 
     def add(way, step, c):
-        which, layer = chunks[c]
         place = place_of(way, block_of(way, step + 2), c)
         ring.send(way, place, place, send_sem.at[way, c], sum_sem.at[way, step, c]).wait_recv()
         term_copy(way, step, c).wait()
-        term = terms[which][way, lax.rem(step, 2), layer]
+        term = terms[c][way, lax.rem(step, 2)]
         total = (place[...].astype(jnp.float32) + term.astype(jnp.float32)).astype(jnp.bfloat16)
         place[...] = total
         return total
@@ -152,7 +146,7 @@
     for c, way in every:
         total = add(way, n - 2, c).astype(jnp.float32)
         square = total * total
-        square = jnp.sum(square.reshape(square.shape[0] // 8, 8, square.shape[1]), axis=0)
+        square = jnp.sum(square.reshape(-1, 8, square.shape[-1]), axis=0)
         for i in range(square.shape[1] // 128):
             tile = tile + square[:, i * 128 : (i + 1) * 128]
     for c, way in every:
@@ -183,22 +177,21 @@
     total = jnp.sum(jnp.sum(squares[...], axis=0), axis=(0, 1), keepdims=True)
     factor = jnp.minimum(1.0, 0.5 * lax.rsqrt(total / count + 1e-30))
 
-    gathered = [(c, way) for c, way in every if chunks[c][0] < 2]
-    for c, way in every:
-        which, layer = chunks[c]
-        here = pl.ds(way * half[which], half[which])
+    gathered = [(c, way) for c, way in every if c < 2]
+    for c, way in every:
+        here = pl.ds(way * half[c], half[c])
         place = place_of(way, me, c)
-        new, m_new[which][layer, here], v_new[which][layer, here] = adamw(
-            w_own[which][layer, here].astype(jnp.float32),
-            m_new[which][layer, here],
-            v_new[which][layer, here],
+        new, m_new[c][:, here], v_new[c][:, here] = adamw(
+            w_own[c][:, here].astype(jnp.float32),
+            m_new[c][:, here],
+            v_new[c][:, here],
             place[...].astype(jnp.float32) * factor,
         )
         if (c, way) in gathered:
             place[...] = new
             ring.send(way, place, place, send_sem.at[way, c], whole_sem.at[way, 0, c]).start()
         else:
-            own_down[layer, here] = new
+            own_down[:, here] = new
     gather(ring, gathered, place_of, send_sem, whole_sem)
     for way in range(WAYS):
         for step in range(hops[way]):
@@ -245,7 +238,7 @@
     def step(*arrays):
         terms, weights, m, v = (arrays[i : i + 3] for i in (0, 3, 6, 9))
         layers = weights[0].shape[0]
-        count = 3 * layers
+        count = len(weights)
         hbm = pl.BlockSpec(memory_space=pltpu.HBM)
         vmem = pl.BlockSpec(memory_space=pltpu.VMEM)
         cut = [(layers, x.shape[1] // n, x.shape[2]) for x in weights]

time: 487 us -> 487 us (level)
  no operation moved by 1% of the time
where the time goes in v4:
time: 487 us
  Pallas kernels  486 us (100%)
    pallas_call x1, Pallas kernels, step(): pl.pallas_call(functools.partial(sum_and_step, n), out_shape=[*(pltpu.VME...  409 us
    pallas_call x1, Pallas kernels, step(): pl.pallas_call(functools.partial(gather_last, n), out_shape=pltpu.VMEM(we...  63.8 us
    pallas_call x2, Pallas kernels, put(): pl.pallas_call(functools.partial(put_out, len(some)), out_shape=[jax.Shap...  13.2 us

profile of v4, /device:TPU:21, one launch (start us, length us, event | category | flops | bytes accessed | tf_op | source)
XLA Modules:
  0.0 487.0 jit_solution(2616860480754553779)
XLA Ops:
  0.6 409.3 %sum_and_step.1 = (bf16[2,512,4096]{2,1,0:T(8,128)(2,1)S(1)}, bf16[2,512,4096]{2,1,0:T(8,128)(2,1)S(1)}, bf16[2,512,512]{2,1,0:T(8,128)(2,1)S(1)}, f32[2,64,4096...) custom-call(bf16[1,2,512,4096]{3,2,1,0:T(8,128)(2,1)} %refs_0_.1, ...), custom_call_target="tpu_custom_call" | custom-call | tf_op jit(solution)/shard_map/sum_and_step/pallas_call | solution.py:247
  410.0 9.8 %put_out.2 = (bf16[2,512,4096]{2,1,0:T(8,128)(2,1)}, bf16[2,512,4096]{2,1,0:T(8,128)(2,1)}, f32[2,64,4096]{2,1,0:T(8,128)}, f32[2,64,4096]{2,1,0:T(8,128)}, f32[...) custom-call(bf16[2,512,4096]{2,1,0:T(8,128)(2,1)S(1)} %get-tuple-ele, ...), custom_call_target="tpu_custom_call" | custom-call | tf_op jit(solution)/shard_map/put_out/pallas_call | solution.py:276
  419.8 63.8 %gather_last.1.refs_0_ = bf16[2,4096,512]{2,1,0:T(8,128)(2,1)S(1)} custom-call(bf16[2,512,512]{2,1,0:T(8,128)(2,1)S(1)} %get-tuple-element.37.new, f32[8,128]{1,0:T(8,128)S(1)} %get-tuple-element.38.after), custom_call_target="tpu_custom_call" | custom-call | tf_op jit(solution)/shard_map/gather_last/pallas_call | solution.py:289
  483.6 3.4 put_out.3

commit v5 on v4

--- a/solution.py
+++ b/solution.py
@@ -93,8 +93,6 @@
     barrier = pltpu.get_barrier_semaphore()
     for to in ring.to:
         pl.semaphore_signal(barrier, inc=1, device_id={"dp": to}, device_id_type=MESH)
-    for c, way in every:
-        term_copy(way, 0, c).start()
     pl.semaphore_wait(barrier, WAYS)
     pl.delay(lax.rem(lax.axis_index("rep"), 2) * LAG)
 
@@ -107,8 +105,9 @@
         src = g[c].at[0, :, rows(c, block, way)]
         ring.send(way, src, place_of(way, block, c), send_sem.at[way, c], sum_sem.at[way, 0, c]).start()
 
-    for c, way in every:
-        term_copy(way, 1, c).start()
+    for step in range(2):
+        for c, way in every:
+            term_copy(way, step, c).start()
     own_loads = []
     for which in range(3):
         mine = pl.ds(pl.multiple_of(me * own[which], own[which]), own[which])

time: 487 us -> 487 us (level)
  no operation moved by 1% of the time
where the time goes in v5:
time: 487 us
  Pallas kernels  486 us (100%)
    pallas_call x1, Pallas kernels, step(): pl.pallas_call(functools.partial(sum_and_step, n), out_shape=[*(pltpu.VME...  409 us
    pallas_call x1, Pallas kernels, step(): pl.pallas_call(functools.partial(gather_last, n), out_shape=pltpu.VMEM(we...  63.8 us
    pallas_call x2, Pallas kernels, put(): pl.pallas_call(functools.partial(put_out, len(some)), out_shape=[jax.Shap...  13.2 us

profile of v5, /device:TPU:21, one launch (start us, length us, event | category | flops | bytes accessed | tf_op | source)
XLA Modules:
  0.0 487.0 jit_solution(17584837981305771498)
XLA Ops:
  0.6 409.3 %sum_and_step.1 = (bf16[2,512,4096]{2,1,0:T(8,128)(2,1)S(1)}, bf16[2,512,4096]{2,1,0:T(8,128)(2,1)S(1)}, bf16[2,512,512]{2,1,0:T(8,128)(2,1)S(1)}, f32[2,64,4096...) custom-call(bf16[1,2,512,4096]{3,2,1,0:T(8,128)(2,1)} %refs_0_.1, ...), custom_call_target="tpu_custom_call" | custom-call | tf_op jit(solution)/shard_map/sum_and_step/pallas_call | solution.py:246
  410.0 9.8 %put_out.2 = (bf16[2,512,4096]{2,1,0:T(8,128)(2,1)}, bf16[2,512,4096]{2,1,0:T(8,128)(2,1)}, f32[2,64,4096]{2,1,0:T(8,128)}, f32[2,64,4096]{2,1,0:T(8,128)}, f32[...) custom-call(bf16[2,512,4096]{2,1,0:T(8,128)(2,1)S(1)} %get-tuple-ele, ...), custom_call_target="tpu_custom_call" | custom-call | tf_op jit(solution)/shard_map/put_out/pallas_call | solution.py:275
  419.8 63.8 %gather_last.1.refs_0_ = bf16[2,4096,512]{2,1,0:T(8,128)(2,1)S(1)} custom-call(bf16[2,512,512]{2,1,0:T(8,128)(2,1)S(1)} %get-tuple-element.37.new, f32[8,128]{1,0:T(8,128)S(1)} %get-tuple-element.38.after), custom_call_target="tpu_custom_call" | custom-call | tf_op jit(solution)/shard_map/gather_last/pallas_call | solution.py:288
  483.6 3.4 put_out.3
